TPU v7x, 32 devices: a whole 2x2x4 slice. The times are simulated.
32 devices in a mesh: row: 4 (over z), col: 8 (over y, x, core).
Axes of the slice: x: 2, y: 2, z: 4, core: 2. Of those that a mesh axis runs over, the one named last changes fastest.
Arguments:
- tokens: bfloat16 [2048, 2048], P(('row', 'col')), may hold values from -6 to 6
- timestep: int32 [1], replicated, may hold values from 0 to 999
- mod_weight: float32 [256, 2048], replicated, may hold values from -0.375 to 0.375
- qkv_weight: bfloat16 [3, 2048, 2048], P(None, None, 'col'), may hold values from -0.125 to 0.125
- attn_scale: float32 [16], P('col'), may hold values from 4 to 40
- out_weight: bfloat16 [2048, 2048], P('col'), may hold values from -0.5 to 0.5
- grad_update: bfloat16 [2048, 2048], P(('row', 'col')), may hold values from -6 to 6
Outputs:
- update: bfloat16 [2048, 2048], P(('row', 'col'))
- grad_tokens: bfloat16 [2048, 2048], P(('row', 'col'))
- grad_qkv: float32 [3, 2048, 2048], P(None, 'row', 'col')
- grad_out: float32 [2048, 2048], P('col', 'row')
All inputs are finite; a program needn't handle non-finite values.
Results may differ from a plain program's by a relative error of at most 0.018.
Values may be sent and summed in bfloat16 or wider, within the bound.
A program may use at most 128 MiB of HBM per device.

v0:
```python
import math
import jax
import jax.numpy as jnp
from jax import lax
from jax.sharding import PartitionSpec as P

epsilon = 1e-06


def embed(timestep, count):
    index = jnp.arange(count, dtype=jnp.float32)
    freqs = jnp.exp(-math.log(10000.0) * index / count)
    angles = timestep.astype(jnp.float32)[0] * freqs
    return jnp.concatenate([jnp.cos(angles), jnp.sin(angles)])


def unit_rows(values):
    factor = lax.rsqrt(jnp.mean(values * values, -1, keepdims=True) + epsilon)
    return (values * factor, factor)


def unit_grad(grad_unit, unit, factor):
    return factor * (grad_unit - unit * jnp.mean(grad_unit * unit, -1, keepdims=True))


def split_blocks(array, size):
    return array.reshape((array.shape[0] // size, size) + array.shape[1:])


def per_device(tokens, timestep, mod_weight, qkv_weight, attn_scale, out_weight, grad_update):
    tok_dev, width = tokens.shape
    heads_here = attn_scale.shape[0]
    inner = qkv_weight.shape[2]
    head_dim = inner // heads_here
    span = tok_dev * lax.axis_size("col")
    coeff = attn_scale / head_dim
    embedded = embed(timestep, mod_weight.shape[0] // 2)
    gain = 1.0 + jnp.sum(embedded[:, None] * mod_weight, 0)
    tok_float = tokens.astype(jnp.float32)
    rstd = lax.rsqrt(jnp.mean(tok_float * tok_float, -1, keepdims=True) + epsilon)
    normed = tok_float * rstd
    hidden = (normed * gain).astype(jnp.bfloat16)
    group = lax.all_gather(hidden, "col", axis=0, tiled=True)
    raw = jnp.einsum("sd,kdh->ksh", group, qkv_weight, preferred_element_type=jnp.float32)
    query_unit, query_factor = unit_rows(raw[0].reshape(span, heads_here, head_dim))
    key_unit, key_factor = unit_rows(raw[1].reshape(span, heads_here, head_dim))
    queries = query_unit.astype(jnp.bfloat16)
    key_heads = key_unit.astype(jnp.bfloat16)
    value_heads = raw[2].astype(jnp.bfloat16).reshape(span, heads_here, head_dim)
    start_state = (
        jnp.zeros((heads_here, span), jnp.float32),
        jnp.zeros((span, heads_here, head_dim), jnp.float32),
    )
    carry = start_state
    key_piece = lax.all_gather(key_heads, "row", axis=0, tiled=True)
    value_piece = lax.all_gather(value_heads, "row", axis=0, tiled=True)
    size = math.gcd(key_piece.shape[0], 512)

    def attend_step(state, block):
        key_block, value_block = block
        scores = (
            jnp.einsum("qhd,khd->hqk", queries, key_block, preferred_element_type=jnp.float32)
            * coeff[:, None, None]
        )
        weights = jnp.exp(scores - attn_scale[:, None, None])
        totals = state[0] + jnp.sum(weights, -1)
        mixed = state[1] + jnp.einsum(
            "hqk,khd->qhd",
            weights.astype(jnp.bfloat16),
            value_block,
            preferred_element_type=jnp.float32,
        )
        return ((totals, mixed), None)

    carry, unused = lax.scan(
        attend_step, carry, (split_blocks(key_piece, size), split_blocks(value_piece, size))
    )
    totals, mixed = carry
    attended_heads = (mixed / totals.T[:, :, None]).astype(jnp.bfloat16)
    attended = attended_heads.reshape(span, inner)
    rows = attended
    update = lax.psum_scatter(
        jnp.dot(rows, out_weight, preferred_element_type=jnp.float32).astype(jnp.bfloat16),
        "col",
        scatter_dimension=0,
        tiled=True,
    )
    grad_group = lax.all_gather(grad_update, "col", axis=0, tiled=True)
    out_part = lax.dot_general(
        attended, grad_group, (((0,), (0,)), ((), ())), preferred_element_type=jnp.float32
    )
    grad_out = lax.psum_scatter(
        out_part.astype(jnp.bfloat16), "row", scatter_dimension=1, tiled=True
    ).astype(jnp.float32)
    grad_attended = lax.dot_general(
        grad_group, out_weight, (((1,), (1,)), ((), ())), preferred_element_type=jnp.float32
    ).astype(jnp.bfloat16)
    grad_heads = grad_attended.reshape(span, heads_here, head_dim)
    delta = jnp.sum(grad_heads.astype(jnp.float32) * attended_heads.astype(jnp.float32), -1)
    inverse = 1.0 / totals

    def pair_terms(query_rows, grad_rows, inverse_rows, delta_rows, key_block, value_block):
        scores = (
            jnp.einsum("qhd,khd->hqk", query_rows, key_block, preferred_element_type=jnp.float32)
            * coeff[:, None, None]
        )
        probs = jnp.exp(scores - attn_scale[:, None, None]) * inverse_rows[:, :, None]
        dprobs = jnp.einsum(
            "qhd,khd->hqk", grad_rows, value_block, preferred_element_type=jnp.float32
        )
        dscores = (probs * (dprobs - delta_rows[:, :, None]) * coeff[:, None, None]).astype(
            jnp.bfloat16
        )
        return (probs, dscores)

    empty_own = jnp.zeros((span, heads_here, head_dim), jnp.float32)
    carry = empty_own
    key_piece = lax.all_gather(key_heads, "row", axis=0, tiled=True)
    value_piece = lax.all_gather(value_heads, "row", axis=0, tiled=True)
    size = math.gcd(key_piece.shape[0], 512)

    def query_step(state, block):
        key_block, value_block = block
        probs, dscores = pair_terms(queries, grad_heads, inverse, delta.T, key_block, value_block)
        return (
            state
            + jnp.einsum("hqk,khd->qhd", dscores, key_block, preferred_element_type=jnp.float32),
            None,
        )

    carry, unused = lax.scan(
        query_step, carry, (split_blocks(key_piece, size), split_blocks(value_piece, size))
    )
    grad_query = carry
    all_inverse, all_delta = (
        lax.all_gather(inverse.T, "row", axis=0, tiled=True),
        lax.all_gather(delta, "row", axis=0, tiled=True),
    )
    carry = (empty_own, empty_own)
    query_piece = lax.all_gather(queries, "row", axis=0, tiled=True)
    grad_piece = lax.all_gather(grad_heads, "row", axis=0, tiled=True)
    count = query_piece.shape[0]
    size = math.gcd(count, 512)

    def key_step(state, block):
        query_block, grad_block, inverse_block, delta_block = block
        probs, dscores = pair_terms(
            query_block, grad_block, inverse_block.T, delta_block.T, key_heads, value_heads
        )
        grad_key = state[0] + jnp.einsum(
            "hqk,qhd->khd", dscores, query_block, preferred_element_type=jnp.float32
        )
        grad_value = state[1] + jnp.einsum(
            "hqk,qhd->khd",
            probs.astype(jnp.bfloat16),
            grad_block,
            preferred_element_type=jnp.float32,
        )
        return ((grad_key, grad_value), None)

    carry, unused = lax.scan(
        key_step,
        carry,
        (
            split_blocks(query_piece, size),
            split_blocks(grad_piece, size),
            split_blocks(all_inverse, size),
            split_blocks(all_delta, size),
        ),
    )
    grad_key, grad_value = carry
    grad_q = (
        unit_grad(grad_query, query_unit, query_factor).astype(jnp.bfloat16).reshape(span, inner)
    )
    grad_k = unit_grad(grad_key, key_unit, key_factor).astype(jnp.bfloat16).reshape(span, inner)
    grad_v = grad_value.astype(jnp.bfloat16).reshape(span, inner)
    grad_raw = jnp.stack([grad_q, grad_k, grad_v])
    qkv_part = jnp.einsum("sd,ksh->kdh", group, grad_raw, preferred_element_type=jnp.float32)
    grad_qkv = lax.psum_scatter(
        qkv_part.astype(jnp.bfloat16), "row", scatter_dimension=1, tiled=True
    ).astype(jnp.float32)
    rows = grad_raw
    grad_hidden = lax.psum_scatter(
        jnp.einsum("ksh,kdh->sd", rows, qkv_weight, preferred_element_type=jnp.float32).astype(
            jnp.bfloat16
        ),
        "col",
        scatter_dimension=0,
        tiled=True,
    ).astype(jnp.float32)
    grad_normed = grad_hidden * gain
    grad_tokens = (
        rstd * (grad_normed - normed * jnp.mean(grad_normed * normed, -1, keepdims=True))
    ).astype(jnp.bfloat16)
    return (update, grad_tokens, grad_qkv, grad_out)


def solution(mesh):
    placed = (
        P(("row", "col"), None),
        P(),
        P(),
        P(None, None, "col"),
        P("col"),
        P("col", None),
        P(("row", "col"), None),
    )
    return jax.shard_map(
        per_device,
        mesh=mesh,
        in_specs=placed,
        out_specs=(
            P(("row", "col"), None),
            P(("row", "col"), None),
            P(None, "row", "col"),
            P("col", "row"),
        ),
        check_vma=False,
    )
```

profile of v0, /device:TPU:0, one launch (start us, length us, event | category | flops | bytes accessed | tf_op | source)
XLA Modules:
  0.0 422.1 jit_solution(2159010349905390229)
XLA Ops:
  11.1 30.6 %all-gather.7.cloned.1.call-done = bf16[512,2048]{1,0:T(8,128)(2,1)} async-done(((bf16[64,2048]{1,0:T(8,128)(2,1)}), bf16[512,2048]{1,0:T(8,128)(2,1)}) %all-gather.7.cloned.1.call-update) | async-done | bytes 2097168 | tf_op jit(solution)/shard_map/all_gather | solution.py:43
  41.7 3.4 fusion.54
  60.4 16.5 %all-gather.9.cloned.1.call-done = bf16[2048,2,128]{0,2,1:T(8,128)(2,1)} async-done(((bf16[512,2,128]{0,2,1:T(8,128)(2,1)}), bf16[2048,2,128]{0,2,1:T(8,128)(2,1)}) %all-gather.9.cloned.1.call-update) | async-done | bytes 1048592 | tf_op jit(solution)/shard_map/all_gather | solution.py:55
  82.3 23.6 %all-gather.11.cloned.1.call-done = bf16[2048,2,128]{0,2,1:T(8,128)(2,1)} async-done(((bf16[512,2,128]{0,2,1:T(8,128)(2,1)}), bf16[2048,2,128]{0,2,1:T(8,128)(2,1)}) %all-gather.11.cloned.1.call-update) | async-done | bytes 1048592 | tf_op jit(solution)/shard_map/all_gather | solution.py:56
  105.9 3.7 copy.32
  109.5 32.0 %while.37 = (s32[]{:T(128)}, f32[2,512]{1,0:T(2,128)S(1)}, f32[512,2,128]{0,2,1:T(8,128)}, bf16[4,512,2,128]{3,1,2,0:T(8,128)(2,1)}, bf16[512,2,128]{2,0,1:T(8,1...) while((s32[]{:T(128)}, f32[2,512]{1,0:T(2,128)S(1)}, ...), condition=%wide.region_6.7_spmd.clone, body=%wide.region_4.6_spmd.clone.sunk | while | flops 271844352 | bytes 8143544 | solution.py:75
  141.5 3.5 multiply_reduce_fusion.3
  151.2 33.2 %while.38 = (s32[]{:T(128)}, f32[512,2,128]{0,2,1:T(8,128)}, bf16[4,512,2,128]{1,3,2,0:T(8,128)(2,1)}, bf16[512,2,128]{2,1,0:T(2,128)(2,1)S(1)}, f32[2]{0:T(128)...) while((s32[]{:T(128)}, f32[512,2,128]{0,2,1:T(8,128)}, ...), condition=%wide.region_10.11_spmd.clone, body=%wide.region_9.10_spmd.clone.sunk | while | flops 406585344 | bytes 7087251 | solution.py:131
  155.9 3.6 fusion.110
  164.1 3.6 fusion.110
  172.4 3.8 fusion.110
  180.8 3.6 fusion.110
  190.8 13.2 %all_gather.33 = f32[2048,2]{0,1:T(2,128)S(1)} all-gather(f32[512,2]{0,1:T(2,128)S(1)} %get-tuple-element.734), channel_id=1, replica_groups=mesh['row'=4,'col'=8] {'row'}, dimensions={0}, use_global_device_ids=true | all-gather | bytes 20480 | tf_op jit(solution)/shard_map/all_gather | solution.py:137
  204.0 13.2 %all_gather.31 = f32[2048,2]{0,1:T(2,128)S(1)} all-gather(f32[512,2]{0,1:T(2,128)S(1)} %fusion.81), channel_id=1, replica_groups=mesh['row'=4,'col'=8] {'row'}, dimensions={0}, use_global_device_ids=true | all-gather | bytes 20480 | tf_op jit(solution)/shard_map/all_gather | solution.py:136
  217.2 3.4 convolution_convert_fusion.2
  220.9 36.4 %while.39 = (s32[]{:T(128)}, f32[512,2,128]{0,2,1:T(8,128)}, f32[512,2,128]{0,2,1:T(8,128)}, bf16[4,512,2,128]{3,1,0,2:T(8,128)(2,1)}, bf16[512,2,128]{2,0,1:T(8...) while((s32[]{:T(128)}, f32[512,2,128]{0,2,1:T(8,128)}, ...), condition=%wide.region_13.14_spmd.clone, body=%wide.region_12.13_spmd.clone.sunk | while | flops 541589504 | bytes 9988260 | solution.py:161
  235.8 3.3 fusion.118
  244.9 3.3 fusion.118
  262.7 4.3 %bitcast_convert_fusion.2 = bf16[512,2048]{1,0:T(8,128)(2,1)} fusion(bf16[3,2048,256]{2,1,0:T(8,128)(2,1)S(1)} %copy-done, bf16[1,512,256]{2,1,0:T(8,128)(2,1)} %copy.59, bf16[1,512,256]{2,1,0:T(8,128)(2,1)} %copy.58, bf16[1,512,256]{2,1,0:T(8,128)(2,1)} %stack_reshape.9), kind=kOutput, calls=%fused_computation.57 | convolution fusion | flops 1612447744 | bytes 6029312 | tf_op jit(solution)/shard_map/ksh,kdh->sd/dot_general | solution.py:184
  268.0 5.2 %fusion.50 = bf16[3,2048,256]{1,2,0:T(8,128)(2,1)} fusion(bf16[512,2048]{1,0:T(8,128)(2,1)} %all-gather.7.cloned.1.call-done, bf16[1,512,256]{2,1,0:T(8,128)(2,1)} %copy.59, bf16[1,512,256]{2,1,0:T(8,128)(2,1)} %copy.58, bf16[1,512,256]{2,1,0:T(8,128)(2,1)S(1)} %copy-done.11), kind=kOutput, calls=%fused_computation.60 | convolution fusion | flops 1612972032 | bytes 6029312 | tf_op jit(solution)/shard_map/sd,ksh->kdh/dot_general | solution.py:178
  274.2 3.4 convolution_convert_fusion.1
  279.5 28.2 %reduce-scatter.7.cloned.1.call-done = bf16[64,2048]{1,0:T(8,128)(2,1)} async-done(((bf16[512,2048]{1,0:T(8,128)(2,1)}), bf16[64,2048]{1,0:T(8,128)(2,1)}) %reduce-scatter.7.cloned.1.call-update) | async-done | bytes 262160 | tf_op jit(solution)/shard_map/reduce_scatter | solution.py:183
  310.8 59.7 %reduce-scatter.9.cloned.1.call-done = bf16[3,512,256]{1,2,0:T(8,128)(2,1)} async-done(((bf16[3,2048,256]{1,2,0:T(8,128)(2,1)}), bf16[3,512,256]{1,2,0:T(8,128)(2,1)}) %reduce-scatter.9.cloned.1.call-update) | async-done | bytes 786448 | tf_op jit(solution)/shard_map/reduce_scatter | solution.py:179
  373.0 42.2 %reduce-scatter.5.cloned.1.call-done = bf16[64,2048]{1,0:T(8,128)(2,1)} async-done(((bf16[512,2048]{1,0:T(8,128)(2,1)}), bf16[64,2048]{1,0:T(8,128)(2,1)}) %reduce-scatter.5.cloned.1.call-update) | async-done | bytes 262160 | tf_op jit(solution)/shard_map/reduce_scatter | solution.py:82
  (147 shorter events, 131.1 us)
Async XLA Ops:
  7.2 34.6 %copy-start = (bf16[3,2048,256]{2,1,0:T(8,128)(2,1)S(1)}, bf16[3,2048,256]{2,1,0:T(8,128)(2,1)}, u32[]{:S(2)}) copy-start(bf16[3,2048,256]{2,1,0:T(8,128)(2,1)} %param.16) | copy-start | bytes 9437188
  7.2 2.9 copy-start.7
  7.2 34.5 %all-gather.7.cloned.1.call-start = ((), (), s32[]{:S(2)}) async-start(), calls=%async_computation.4 | async-start | bytes 2359296 | tf_op jit(solution)/shard_map/all_gather | solution.py:43
  11.1 65.8 %all-gather.9.cloned.1.call-start = ((), (), s32[]{:S(2)}) async-start(), calls=%async_computation.5 | async-start | bytes 1310720 | tf_op jit(solution)/shard_map/all_gather | solution.py:55
  45.2 1.1 copy-start.10
  46.3 5.0 %copy-start.12 = (f32[2]{0:T(128)S(1)}, f32[2]{0:T(128)}, u32[]{:S(2)}) copy-start(f32[2]{0:T(128)} %param.17) | copy-start | bytes 28
  48.8 57.1 %all-gather.11.cloned.1.call-start = ((), (), s32[]{:S(2)}) async-start(), calls=%async_computation.6 | async-start | bytes 1310720 | tf_op jit(solution)/shard_map/all_gather | solution.py:56
  50.6 90.9 %all-gather.13.cloned.1.call-start = ((), (), s32[]{:S(2)}) async-start(), calls=%async_computation.8 | async-start | bytes 2359296 | tf_op jit(solution)/shard_map/all_gather | solution.py:88
  51.2 169.7 %all-gather.15.cloned.1.call-start = ((), (), s32[]{:S(2)}) async-start(), calls=%async_computation.9 | async-start | bytes 1310720 | tf_op jit(solution)/shard_map/all_gather | solution.py:140
  59.4 1.0 copy-start.1
  60.4 160.5 %all-gather.17.cloned.1.call-start = ((), (), s32[]{:S(2)}) async-start(), calls=%async_computation.10 | async-start | bytes 1310720 | tf_op jit(solution)/shard_map/all_gather | solution.py:141
  79.5 30.0 %copy-start.2 = (bf16[512,2,128]{2,0,1:T(8,128)(2,1)S(1)}, bf16[512,2,128]{2,0,1:T(8,128)(2,1)}, u32[]{:S(2)}) copy-start(bf16[512,2,128]{2,0,1:T(8,128)(2,1)} %copy-done.1) | copy-start | bytes 786436
  114.3 3.2 copy-start.3
  122.3 3.2 copy-start.3
  130.3 3.2 copy-start.3
  138.3 3.2 copy-start.3
  145.1 6.1 %copy-start.6 = (bf16[512,2,128]{2,1,0:T(2,128)(2,1)S(1)}, bf16[512,2,128]{2,1,0:T(2,128)(2,1)}, u32[]{:S(2)}) copy-start(bf16[512,2,128]{2,1,0:T(2,128)(2,1)} %copy.36) | copy-start | bytes 786436
  151.2 126.4 %reduce-scatter.11.cloned.1.call-start = ((), (), s32[]{:S(2)}) async-start(), calls=%async_computation.13 | async-start | bytes 1310720 | tf_op jit(solution)/shard_map/reduce_scatter | solution.py:92
  217.2 3.7 copy-start.5
  220.7 87.1 %reduce-scatter.7.cloned.1.call-start = ((), (), s32[]{:S(2)}) async-start(), calls=%async_computation.11 | async-start | bytes 2359296 | tf_op jit(solution)/shard_map/reduce_scatter | solution.py:183
  267.1 103.4 %reduce-scatter.9.cloned.1.call-start = ((), (), s32[]{:S(2)}) async-start(), calls=%async_computation.12 | async-start | bytes 3932160 | tf_op jit(solution)/shard_map/reduce_scatter | solution.py:179
  273.2 1.0 copy-start.9
  273.3 142.0 %reduce-scatter.5.cloned.1.call-start = ((), (), s32[]{:S(2)}) async-start(), calls=%async_computation.7 | async-start | bytes 2359296 | tf_op jit(solution)/shard_map/reduce_scatter | solution.py:82
  277.6 30.2 %copy-start.8 = (bf16[64,2048]{1,0:T(8,128)(2,1)S(1)}, bf16[64,2048]{1,0:T(8,128)(2,1)}, u32[]{:S(2)}) copy-start(bf16[64,2048]{1,0:T(8,128)(2,1)} %param.13) | copy-start | bytes 786436
  (2 other events, 1.8 us)
Sparse Core Ops, SparseCore 0:
  11.2 30.4 all-gather.6
  48.9 27.9 all-gather.8
  78.5 27.3 all-gather.10
  107.6 27.1 all-gather.12
  136.8 28.0 all-gather.14
  166.3 27.3 all-gather.16
  220.8 26.5 reduce-scatter.10
  267.2 40.4 reduce-scatter.6
  310.0 60.3 reduce-scatter.8
  374.2 41.0 reduce-scatter.4
where the time goes:
time: 424 us; the launch traced here: 422 us
  waiting for transfers between devices  202 us (48%)
  matrix products  109 us (26%)
  local copies, waits for them, and re-layouts  50.9 us (12%)
  blocking collectives  26.4 us (6%)
  other arithmetic  17.9 us (4%)
  between operations  15.3 us (4%)
    reduce_scatter x1, waiting for transfers between devices, per_device(): lax.psum_scatter(qkv_part.astype(jnp.bfloat16), 'row', scatter_dimension=...  59.7 us
    reduce_scatter x1, waiting for transfers between devices, per_device(): lax.psum_scatter(jnp.dot(rows, out_weight, preferred_element_type=jnp.flo...  42.2 us
    all_gather x1, waiting for transfers between devices, per_device(): group = lax.all_gather(hidden, 'col', axis=0, tiled=True)  30.6 us
    reduce_scatter x1, waiting for transfers between devices, per_device(): lax.psum_scatter(jnp.einsum('ksh,kdh->sd', rows, qkv_weight, preferred_el...  28.2 us
    all_gather x1, waiting for transfers between devices, per_device(): value_piece = lax.all_gather(value_heads, 'row', axis=0, tiled=True)  23.6 us
    dot_general x8, matrix products, pair_terms(): jnp.einsum('qhd,khd->hqk', query_rows, key_block, preferred_element_type=...  22.8 us
    all_gather x1, waiting for transfers between devices, per_device(): key_piece = lax.all_gather(key_heads, 'row', axis=0, tiled=True)  16.5 us
    unnamed x30, local copies, waits for them, and re-layouts  15.4 us
  transfers between devices with their start and end apart: 10, of which 6 were waited for; matrix products, arithmetic and copies ran while one was open for 39% of the time, Pallas kernels for 0%

commit v1 on v0

--- a/solution.py
+++ b/solution.py
@@ -52,8 +52,13 @@
         jnp.zeros((span, heads_here, head_dim), jnp.float32),
     )
     carry = start_state
-    key_piece = lax.all_gather(key_heads, "row", axis=0, tiled=True)
-    value_piece = lax.all_gather(value_heads, "row", axis=0, tiled=True)
+    key_piece, value_piece = jnp.split(
+        lax.all_gather(
+            jnp.concatenate([key_heads, value_heads], axis=1), "row", axis=0, tiled=True
+        ),
+        [key_heads.shape[1]],
+        axis=1,
+    )
     size = math.gcd(key_piece.shape[0], 512)
 
     def attend_step(state, block):

time: 424 us -> 466 us (1.099)
  waiting for transfers between devices: 202 us -> 247 us
    all_gather x0 -> x1, waiting for transfers between devices: none -> 43.4 us  [per_device(): lax.all_gather(jnp.concatenate([key_heads, value_heads], axis=1), 'row',...]
    dynamic_slice x8 -> x0, local copies, waits for them, and re-layouts: 8 us -> none  [per_device(): lax.scan(attend_step, carry, (split_blocks(key_piece, size), split_blocks...]
    unnamed x30 -> x33, local copies, waits for them, and re-layouts: 15.4 us -> 17 us
  transfers between devices with their start and end apart: 10 -> 11, of which waited for: 6 -> 7; matrix products, arithmetic and copies ran while one was open for 39% -> 35% of each run, Pallas kernels for 0% -> 0%
where the time goes in v1:
time: 466 us; the launch traced here: 464 us
  waiting for transfers between devices  247 us (53%)
  matrix products  109 us (23%)
  local copies, waits for them, and re-layouts  46.4 us (10%)
  blocking collectives  26.6 us (6%)
  other arithmetic  19.8 us (4%)
  between operations  15 us (3%)
    reduce_scatter x1, waiting for transfers between devices, per_device(): lax.psum_scatter(qkv_part.astype(jnp.bfloat16), 'row', scatter_dimension=...  59.5 us
    all_gather x1, waiting for transfers between devices, per_device(): lax.all_gather(jnp.concatenate([key_heads, value_heads], axis=1), 'row',...  43.4 us
    reduce_scatter x1, waiting for transfers between devices, per_device(): lax.psum_scatter(jnp.dot(rows, out_weight, preferred_element_type=jnp.flo...  42.4 us
    all_gather x1, waiting for transfers between devices, per_device(): group = lax.all_gather(hidden, 'col', axis=0, tiled=True)  30.6 us
    reduce_scatter x1, waiting for transfers between devices, per_device(): lax.psum_scatter(jnp.einsum('ksh,kdh->sd', rows, qkv_weight, preferred_el...  27.5 us
    all_gather x1, waiting for transfers between devices, per_device(): value_piece = lax.all_gather(value_heads, 'row', axis=0, tiled=True)  27.2 us
    dot_general x8, matrix products, pair_terms(): jnp.einsum('qhd,khd->hqk', query_rows, key_block, preferred_element_type=...  22.7 us
    unnamed x33, local copies, waits for them, and re-layouts  17 us
  transfers between devices with their start and end apart: 11, of which 7 were waited for; matrix products, arithmetic and copies ran while one was open for 35% of the time, Pallas kernels for 0%

profile of v1, /device:TPU:0, one launch (start us, length us, event | category | flops | bytes accessed | tf_op | source)
XLA Modules:
  0.0 464.2 jit_solution(14620670859042457299)
XLA Ops:
  11.1 30.6 %all-gather.8.cloned.1.call-done = bf16[512,2048]{1,0:T(8,128)(2,1)} async-done(((bf16[64,2048]{1,0:T(8,128)(2,1)}), bf16[512,2048]{1,0:T(8,128)(2,1)}) %all-gather.8.cloned.1.call-update) | async-done | bytes 2097168 | tf_op jit(solution)/shard_map/all_gather | solution.py:43
  41.7 3.4 fusion.56
  60.4 15.4 %all-gather.12.cloned.1.call-done = bf16[2048,2,128]{0,2,1:T(8,128)(2,1)} async-done(((bf16[512,2,128]{0,2,1:T(8,128)(2,1)}), bf16[2048,2,128]{0,2,1:T(8,128)(2,1)}) %all-gather.12.cloned.1.call-update) | async-done | bytes 1048592 | tf_op jit(solution)/shard_map/all_gather | solution.py:123
  78.2 27.2 %all-gather.14.cloned.1.call-done = bf16[2048,2,128]{0,2,1:T(8,128)(2,1)} async-done(((bf16[512,2,128]{0,2,1:T(8,128)(2,1)}), bf16[2048,2,128]{0,2,1:T(8,128)(2,1)}) %all-gather.14.cloned.1.call-update) | async-done | bytes 1048592 | tf_op jit(solution)/shard_map/all_gather | solution.py:124
  105.4 3.7 copy.58
  109.1 43.4 %all-gather.10.cloned.1.call-done = bf16[2048,4,128]{0,2,1:T(8,128)(2,1)} async-done(((bf16[512,4,128]{0,2,1:T(8,128)(2,1)}), bf16[2048,4,128]{0,2,1:T(8,128)(2,1)}) %all-gather.10.cloned.1.call-update) | async-done | bytes 2097168 | tf_op jit(solution)/shard_map/all_gather | solution.py:56
  163.4 23.6 %while.37 = (s32[]{:T(128)}, f32[2,512]{1,0:T(2,128)S(1)}, f32[512,2,128]{0,2,1:T(8,128)}, bf16[4,512,2,128]{3,1,2,0:T(8,128)(2,1)}, bf16[512,2,128]{2,0,1:T(8,1...) while((s32[]{:T(128)}, f32[2,512]{1,0:T(2,128)S(1)}, ...), condition=%wide.region_6.7_spmd.clone, body=%wide.region_4.6_spmd.clone.sunk | while | flops 271844352 | bytes 6046864 | solution.py:80
  187.0 3.6 multiply_reduce_fusion.3
  194.3 33.0 %while.38 = (s32[]{:T(128)}, f32[512,2,128]{0,2,1:T(8,128)}, bf16[4,512,2,128]{1,3,2,0:T(8,128)(2,1)}, bf16[512,2,128]{2,1,0:T(2,128)(2,1)S(1)}, f32[2]{0:T(128)...) while((s32[]{:T(128)}, f32[512,2,128]{0,2,1:T(8,128)}, ...), condition=%wide.region_10.11_spmd.clone, body=%wide.region_9.10_spmd.clone.sunk | while | flops 406585344 | bytes 7087251 | solution.py:136
  199.0 3.6 fusion.113
  207.2 3.6 fusion.113
  215.5 3.6 fusion.113
  223.7 3.7 fusion.113
  233.7 13.4 %all_gather.35 = f32[2048,2]{0,1:T(2,128)S(1)} all-gather(f32[512,2]{0,1:T(2,128)S(1)} %get-tuple-element.731), channel_id=1, replica_groups=mesh['row'=4,'col'=8] {'row'}, dimensions={0}, use_global_device_ids=true | all-gather | bytes 20480 | tf_op jit(solution)/shard_map/all_gather | solution.py:142
  247.1 13.2 %all_gather.33 = f32[2048,2]{0,1:T(2,128)S(1)} all-gather(f32[512,2]{0,1:T(2,128)S(1)} %fusion.84), channel_id=1, replica_groups=mesh['row'=4,'col'=8] {'row'}, dimensions={0}, use_global_device_ids=true | all-gather | bytes 20480 | tf_op jit(solution)/shard_map/all_gather | solution.py:141
  260.3 3.4 convolution_convert_fusion.2
  264.0 36.5 %while.39 = (s32[]{:T(128)}, f32[512,2,128]{0,2,1:T(8,128)}, f32[512,2,128]{0,2,1:T(8,128)}, bf16[4,512,2,128]{3,1,0,2:T(8,128)(2,1)}, bf16[512,2,128]{2,0,1:T(8...) while((s32[]{:T(128)}, f32[512,2,128]{0,2,1:T(8,128)}, ...), condition=%wide.region_13.14_spmd.clone, body=%wide.region_12.13_spmd.clone.sunk | while | flops 541589504 | bytes 9988260 | solution.py:166
  279.0 3.3 fusion.121
  305.9 4.3 bitcast_convert_fusion.2
  311.2 5.3 %fusion.52 = bf16[3,2048,256]{1,2,0:T(8,128)(2,1)} fusion(bf16[512,2048]{1,0:T(8,128)(2,1)} %all-gather.8.cloned.1.call-done, bf16[1,512,256]{2,1,0:T(8,128)(2,1)} %copy.60, bf16[1,512,256]{2,1,0:T(8,128)(2,1)} %copy.59, bf16[1,512,256]{2,1,0:T(8,128)(2,1)S(1)} %copy-done.11), kind=kOutput, calls=%fused_computation.61 | convolution fusion | flops 1612972032 | bytes 6029312 | tf_op jit(solution)/shard_map/sd,ksh->kdh/dot_general | solution.py:183
  317.4 3.4 convolution_convert_fusion.1
  322.7 27.5 %reduce-scatter.7.cloned.1.call-done = bf16[64,2048]{1,0:T(8,128)(2,1)} async-done(((bf16[512,2048]{1,0:T(8,128)(2,1)}), bf16[64,2048]{1,0:T(8,128)(2,1)}) %reduce-scatter.7.cloned.1.call-update) | async-done | bytes 262160 | tf_op jit(solution)/shard_map/reduce_scatter | solution.py:188
  353.2 59.5 %reduce-scatter.9.cloned.1.call-done = bf16[3,512,256]{1,2,0:T(8,128)(2,1)} async-done(((bf16[3,2048,256]{1,2,0:T(8,128)(2,1)}), bf16[3,512,256]{1,2,0:T(8,128)(2,1)}) %reduce-scatter.9.cloned.1.call-update) | async-done | bytes 786448 | tf_op jit(solution)/shard_map/reduce_scatter | solution.py:184
  415.3 42.4 %reduce-scatter.5.cloned.1.call-done = bf16[64,2048]{1,0:T(8,128)(2,1)} async-done(((bf16[512,2048]{1,0:T(8,128)(2,1)}), bf16[64,2048]{1,0:T(8,128)(2,1)}) %reduce-scatter.5.cloned.1.call-update) | async-done | bytes 262160 | tf_op jit(solution)/shard_map/reduce_scatter | solution.py:87
  (139 shorter events, 131.7 us)
Async XLA Ops:
  7.2 34.6 %copy-start = (bf16[3,2048,256]{2,1,0:T(8,128)(2,1)S(1)}, bf16[3,2048,256]{2,1,0:T(8,128)(2,1)}, u32[]{:S(2)}) copy-start(bf16[3,2048,256]{2,1,0:T(8,128)(2,1)} %param.16) | copy-start | bytes 9437188
  7.2 2.9 copy-start.6
  7.2 34.5 %all-gather.8.cloned.1.call-start = ((), (), s32[]{:S(2)}) async-start(), calls=%async_computation.4 | async-start | bytes 2359296 | tf_op jit(solution)/shard_map/all_gather | solution.py:43
  11.1 64.8 %all-gather.12.cloned.1.call-start = ((), (), s32[]{:S(2)}) async-start(), calls=%async_computation.7 | async-start | bytes 1310720 | tf_op jit(solution)/shard_map/all_gather | solution.py:123
  45.2 1.3 copy-start.10
  46.1 0.8 copy-start.3
  46.1 6.1 %copy-start.12 = (f32[2]{0:T(128)S(1)}, f32[2]{0:T(128)}, u32[]{:S(2)}) copy-start(f32[2]{0:T(128)} %param.17) | copy-start | bytes 28
  47.7 4.5 copy-start.8
  47.7 57.7 %all-gather.14.cloned.1.call-start = ((), (), s32[]{:S(2)}) async-start(), calls=%async_computation.8 | async-start | bytes 1310720 | tf_op jit(solution)/shard_map/all_gather | solution.py:124
  49.6 102.9 %all-gather.10.cloned.1.call-start = ((), (), s32[]{:S(2)}) async-start(), calls=%async_computation.5 | async-start | bytes 2621440 | tf_op jit(solution)/shard_map/all_gather | solution.py:56
  51.5 135.5 %all-gather.16.cloned.1.call-start = ((), (), s32[]{:S(2)}) async-start(), calls=%async_computation.9 | async-start | bytes 2359296 | tf_op jit(solution)/shard_map/all_gather | solution.py:93
  52.1 211.8 %all-gather.18.cloned.1.call-start = ((), (), s32[]{:S(2)}) async-start(), calls=%async_computation.10 | async-start | bytes 1310720 | tf_op jit(solution)/shard_map/all_gather | solution.py:145
  59.3 1.0 copy-start.1
  60.4 203.6 %all-gather.20.cloned.1.call-start = ((), (), s32[]{:S(2)}) async-start(), calls=%async_computation.11 | async-start | bytes 1310720 | tf_op jit(solution)/shard_map/all_gather | solution.py:146
  158.3 5.1 %copy-start.2 = (bf16[512,2,128]{2,0,1:T(8,128)(2,1)S(1)}, bf16[512,2,128]{2,0,1:T(8,128)(2,1)}, u32[]{:S(2)}) copy-start(bf16[512,2,128]{2,0,1:T(8,128)(2,1)} %copy-done.1) | copy-start | bytes 786436
  187.0 7.3 %copy-start.5 = (bf16[512,2,128]{2,1,0:T(2,128)(2,1)S(1)}, bf16[512,2,128]{2,1,0:T(2,128)(2,1)}, u32[]{:S(2)}) copy-start(bf16[512,2,128]{2,1,0:T(2,128)(2,1)} %copy.35) | copy-start | bytes 786436
  194.3 126.5 %reduce-scatter.11.cloned.1.call-start = ((), (), s32[]{:S(2)}) async-start(), calls=%async_computation.14 | async-start | bytes 1310720 | tf_op jit(solution)/shard_map/reduce_scatter | solution.py:97
  260.3 3.7 copy-start.4
  263.7 86.5 %reduce-scatter.7.cloned.1.call-start = ((), (), s32[]{:S(2)}) async-start(), calls=%async_computation.12 | async-start | bytes 2359296 | tf_op jit(solution)/shard_map/reduce_scatter | solution.py:188
  310.2 0.9 copy-start.11
  310.2 102.5 %reduce-scatter.9.cloned.1.call-start = ((), (), s32[]{:S(2)}) async-start(), calls=%async_computation.13 | async-start | bytes 3932160 | tf_op jit(solution)/shard_map/reduce_scatter | solution.py:184
  316.4 1.0 copy-start.9
  316.5 141.2 %reduce-scatter.5.cloned.1.call-start = ((), (), s32[]{:S(2)}) async-start(), calls=%async_computation.6 | async-start | bytes 2359296 | tf_op jit(solution)/shard_map/reduce_scatter | solution.py:87
  320.8 29.4 %copy-start.7 = (bf16[64,2048]{1,0:T(8,128)(2,1)S(1)}, bf16[64,2048]{1,0:T(8,128)(2,1)}, u32[]{:S(2)}) copy-start(bf16[64,2048]{1,0:T(8,128)(2,1)} %param.13) | copy-start | bytes 786436
Sparse Core Ops, SparseCore 0:
  11.2 30.4 all-gather.7
  47.8 27.9 all-gather.11
  78.0 27.3 all-gather.13
  107.4 45.0 all-gather.9
  154.2 26.5 all-gather.15
  182.2 27.9 all-gather.17
  211.8 27.4 all-gather.19
  263.8 25.8 reduce-scatter.10
  310.4 39.7 reduce-scatter.6
  352.3 60.3 reduce-scatter.8
  416.6 40.9 reduce-scatter.4
